TPU v7x, 32 devices: a whole 2x2x4 slice. The times are simulated.
32 devices in a mesh: band: 4 (over y, core), col: 8 (over z, x).
Axes of the slice: x: 2, y: 2, z: 4, core: 2. Of those that a mesh axis runs over, the one named last changes fastest.
Arguments:
- source: bfloat16 [6, 524288], P(None, ('band', 'col')), may hold values from -6 to 6
- weights: bfloat16 [8192, 128, 128], P(('band', 'col')), may hold values from -0.5 to 0.5
- source_block: int32 [8192], P(('band', 'col')), may hold values from 0 to 127
- owner_device: int32 [8192, 1], P(('band', 'col')), may hold values from 0 to 31, as said below
- target_tile: int32 [8192], P(('band', 'col')), may hold values from 0 to 112, as said below
- cutoff: int32 [64], P(('band', 'col')), may hold values from 1 to 511
Outputs:
- remapped: float32 [6, 64, 7200], P(None, 'band', 'col')
- filtered: float32 [6, 64, 7200], P(None, 'band', 'col')
Inputs may be any that keep to these rules, and one draw needn't show every extreme that they name: `owner_device`: owners are numbered band index times 8 plus col index. A device's blocks go only to owners in its own band or in the bands next to it. Among the 256 blocks of one device at most 24 share an owner; in every device exactly 24 do for some owner of its own band, and exactly 24 for some owner of each band next to its own; every device sends at least 15 blocks to each owner of its own band. `target_tile`: every tile of every owner receives at least one block.
All inputs are finite; a program needn't handle non-finite values.
Results may differ from a plain program's by a relative error of at most 0.0003.
Values sent between devices are 32-bit elements; how exact they have to be, the bound alone decides.
A program may use at most 64 MiB of HBM per device.

v0:
```python
import jax
import jax.numpy as jnp
from jax import lax
from jax.sharding import PartitionSpec as P

NLON = 7200
KW = 512
TWO_PI = 6.283185307179586


def extended(array, sides, width):
    for axis, dim in sides:
        size, length = (lax.axis_size(axis), array.shape[dim])
        up = [(i, (i + 1) % size) for i in range(size - 1)]
        down = [(j, i) for i, j in up]
        last = lax.slice_in_dim(array, length - width, length, axis=dim)
        leading = lax.slice_in_dim(array, 0, width, axis=dim)
        before = lax.ppermute(last, axis, up)
        after = lax.ppermute(leading, axis, down)
        array = jnp.concatenate([before, array, after], axis=dim)
    return array


def zonal_table(start_index, length, period, wave_count):
    positions = start_index + lax.broadcasted_iota(jnp.int32, (length, wave_count), 0)
    wave_index = lax.broadcasted_iota(jnp.int32, (length, wave_count), 1)
    phases = positions * wave_index % period
    angles = phases.astype(jnp.float32) * (TWO_PI / period)
    return jnp.concatenate([jnp.cos(angles), jnp.sin(angles)], axis=1)


def spectral_weights(cutoffs, wave_count, period):
    wave_index = lax.broadcasted_iota(jnp.int32, (cutoffs.shape[0], wave_count), 1)
    scaled = jnp.where(wave_index == 0, 1.0, 2.0) / period
    retained = jnp.where(wave_index <= cutoffs[:, None], scaled, 0.0).astype(jnp.float32)
    return jnp.concatenate([retained, retained], axis=1)


def local(source, weights, source_block, owner_device, target_tile, cutoff):
    col_count = lax.axis_size("col")
    levels = source.shape[0]
    block_count = weights.shape[0]
    block_width = weights.shape[1]
    lat_here = cutoff.shape[0]
    lat_band = lat_here * col_count
    longitudes_here = NLON // col_count
    cell_count = lat_band * longitudes_here
    tile_count = (cell_count + block_width - 1) // block_width
    regular = (tile_count + col_count - 1) // col_count
    capacity = regular + max(
        1, (block_count - col_count * regular + 2 * col_count - 1) // (2 * col_count)
    )
    slot_total = 3 * col_count * capacity
    blocks_here = source.reshape(levels, -1, block_width)
    picked = jnp.take(blocks_here, source_block, axis=1)
    partial_value = jnp.einsum("lnb,nbt->nlt", picked, weights, preferred_element_type=jnp.float32)
    tile_rows = jnp.broadcast_to(
        target_tile.astype(jnp.float32)[:, None, None], (block_count, 1, block_width)
    )
    tagged = jnp.concatenate([partial_value, tile_rows], axis=1)
    owners = owner_device[:, 0]
    owner_band = owners // col_count
    owner_col = owners % col_count
    offset = owner_band - lax.axis_index("band") + 1
    row_index = lax.broadcasted_iota(jnp.int32, (block_count, block_count), 0)
    column_index = lax.broadcasted_iota(jnp.int32, (block_count, block_count), 1)
    earlier = (owners[None, :] == owners[:, None]) & (column_index < row_index)
    rank_within = jnp.sum(earlier.astype(jnp.int32), axis=1)
    slot_index = (offset * col_count + owner_col) * capacity + rank_within
    placing = lax.broadcasted_iota(jnp.int32, (slot_total, block_count), 0) == slot_index[None, :]
    outgoing = jnp.dot(
        placing.astype(jnp.float32),
        tagged.reshape(block_count, (levels + 1) * block_width),
        precision=lax.Precision.HIGHEST,
        preferred_element_type=jnp.float32,
    )
    outgoing = outgoing.reshape(3, col_count, capacity, levels + 1, block_width)
    rimmed = extended(jnp.stack([outgoing[0], outgoing[2]]), (("band", 0),), 1)
    arranged = jnp.stack([rimmed[0], outgoing[1], rimmed[3]])
    received = lax.all_to_all(arranged, "col", split_axis=1, concat_axis=1, tiled=True)
    slot_rows = received.reshape(-1, levels + 1, block_width)
    slot_owned = slot_rows[:, levels, 0].astype(jnp.int32)
    slot_data = slot_rows[:, :levels, :].reshape(-1, levels * block_width)
    chooser = (
        lax.broadcasted_iota(jnp.int32, (tile_count, slot_owned.shape[0]), 0) == slot_owned[None, :]
    ).astype(jnp.float32)
    summed = jnp.dot(
        chooser, slot_data, precision=lax.Precision.HIGHEST, preferred_element_type=jnp.float32
    )
    summed = jnp.transpose(summed.reshape(tile_count, levels, block_width), (1, 0, 2)).reshape(
        levels, tile_count * block_width
    )
    remapped = summed[:, :cell_count].reshape(levels, lat_band, longitudes_here)
    retained = spectral_weights(cutoff, KW, NLON)
    local_table = zonal_table(lax.axis_index("col") * longitudes_here, longitudes_here, NLON, KW)
    partial_spectra = jnp.dot(
        remapped.reshape(levels * lat_band, longitudes_here),
        local_table,
        precision=lax.Precision.HIGHEST,
        preferred_element_type=jnp.float32,
    )
    partial_spectra = partial_spectra.reshape(levels, lat_band, 2 * KW)
    spectrum = lax.psum_scatter(partial_spectra, "col", scatter_dimension=1, tiled=True)
    spectrum = spectrum * retained[None]
    band_spectra = lax.all_gather(spectrum, "col", axis=1, tiled=True)
    filtered = jnp.dot(
        band_spectra.reshape(levels * lat_band, 2 * KW),
        local_table.T,
        precision=lax.Precision.HIGHEST,
        preferred_element_type=jnp.float32,
    )
    filtered = filtered.reshape(levels, lat_band, longitudes_here)
    return (remapped, filtered)


def solution(mesh):
    in_specs = (
        P(None, ("band", "col")),
        P(("band", "col"), None, None),
        P(("band", "col")),
        P(("band", "col"), None),
        P(("band", "col")),
        P(("band", "col")),
    )
    out_specs = (P(None, "band", "col"), P(None, "band", "col"))
    return jax.shard_map(local, mesh=mesh, in_specs=in_specs, out_specs=out_specs, check_vma=False)
```

profile of v0, /device:TPU:0, one launch (start us, length us, event | category | flops | bytes accessed | tf_op | source)
XLA Modules:
  0.0 208.3 jit_solution(2805658013106343612)
XLA Ops:
  7.2 0.0 copy-start
  7.2 0.7 compare_and_fusion
  7.9 0.7 compare_select_fusion.1
  8.6 0.9 convert_reduce_fusion
  9.5 0.7 convert_element_type.22
  10.2 0.0 copy-done
  10.2 0.8 gather_fusion
  11.0 4.7 %fusion.12 = f32[256,6,128]{2,1,0:T(8,128)S(1)} fusion(bf16[256,128,128]{2,1,0:T(8,128)(2,1)} %param.7, bf16[256,6,128]{2,1,0:T(8,128)(2,1)S(1)} %gather_fusion, pred[256]{0:T(512)(128)(4,1)S(1)} %compare_and_fusion), kind=kOutput, calls=%fused_computation.20 | convolution fusion | flops 50528256 | bytes 9568512 | tf_op jit(solution)/shard_map/lnb,nbt->nlt/dot_general | solution.py:56
  15.8 0.3 broadcast_in_dim.37
  16.1 0.0 copy-start.2
  16.1 0.2 pad_maximum_fusion.1
  16.4 0.4 copy.32
  16.7 0.1 copy-done.2
  16.8 1.2 fusion.11
  18.0 0.1 fusion.29
  18.2 0.1 slice.28
  18.3 0.1 copy.33
  18.4 3.3 %collective-permute-start = (f32[1,8,24,7,128]{4,2,3,1,0:T(8,128)S(1)}, f32[1,8,24,7,128]{4,2,3,1,0:T(8,128)}, u32[]{:S(2)}, u32[]{:S(2)}) collective-permute-start(f32[1,8,24,7,128]{4,2,3,1,0:T(8,128)S(1)} %copy.33), channel_id=1, source_target_pairs={{0,8},{8,16},{16,24},{1,9},{9,17},{17,25},{2,10},{10,18},{18,26},{... | collective-permute-start | bytes 2064392 | tf_op jit(solution)/shard_map/ppermute | solution.py:18
  21.7 0.1 slice.32
  21.8 0.1 copy.34
  21.9 1.3 collective-permute-start.1
  23.2 0.1 slice.30
  23.3 0.0 collective-permute-done
  23.3 1.2 copy.35
  24.6 2.8 %collective-permute-done.1 = f32[1,8,24,7,128]{4,2,3,1,0:T(8,128)} collective-permute-done((f32[1,8,24,7,128]{4,2,3,1,0:T(8,128)S(1)}, f32[1,8,24,7,128]{4,2,3,1,0:T(8,128)}, u32[]{:S(2)}, u32[]{:S(2)}) %collective-permute-start.1) | collective-permute-done | bytes 688160 | tf_op jit(solution)/shard_map/ppermute | solution.py:19
  27.4 1.2 copy.36
  28.6 0.2 pad_maximum_fusion
  28.9 1.7 copy.37
  30.5 5.9 %all-to-all-start = ((f32[3,8,24,7,128]{4,2,3,0,1:T(8,128)}), f32[3,8,24,7,128]{4,2,3,0,1:T(8,128)}, u32[]{:S(2)}, u32[]{:S(2)}) async-start(f32[3,8,24,7,128]{4,2,3,0,1:T(8,128)} %copy.37), calls=%async_computation | async-start | bytes 4128768 | tf_op jit(solution)/shard_map/all_to_all | solution.py:80
  36.4 0.0 all-reduce.3.cloned.1.call-start
  36.5 0.0 copy-done.4
  36.5 0.6 dynamic-slice
  37.8 8.8 %fusion.7 = (f32[900,512]{1,0:T(8,128)S(1)}, f32[900,512]{1,0:T(8,128)}) fusion(s32[900]{0:T(1024)S(1)} %iota_add_fusion), kind=kLoop, calls=%fused_computation.12 | loop fusion | flops 4147200 | bytes 3690000 | tf_op jit(solution)/shard_map/cos | solution.py:29
  46.6 35.3 %all-to-all-done = f32[3,8,24,7,128]{4,2,3,0,1:T(8,128)} async-done(((f32[3,8,24,7,128]{4,2,3,0,1:T(8,128)}), f32[3,8,24,7,128]{4,2,3,0,1:T(8,128)}, u32[]{:S(2)}, u32[]{:S(2)}) %all-to-all-start) | async-done | bytes 2064416 | tf_op jit(solution)/shard_map/all_to_all | solution.py:80
  81.9 1.8 copy.38
  83.7 0.2 fusion.17
  83.9 0.9 fusion.10
  84.8 0.1 copy.52
  84.9 0.3 reshape.113
  85.2 0.0 copy-start.1
  85.2 0.0 copy-start.3
  85.2 4.7 %fusion.1 = f32[6,16,1024]{2,1,0:T(8,128)} fusion(f32[6,16,900]{2,1,0:T(8,128)S(1)} %reshape.113, f32[900,512]{1,0:T(8,128)} %get-tuple-element.6, f32[900,512]{1,0:T(8,128)S(1)} %get-tuple-element.5), kind=kOutput, calls=%fused_computation.3 | convolution fusion | flops 1062604800 | bytes 4425216 | tf_op jit(solution)/shard_map/dot_general | solution.py:96
  89.9 0.0 all-reduce.3.cloned.1.call-update
  90.0 0.1 compare_select_fusion
  90.0 73.0 %all-reduce.3.cloned.1.call-done = f32[6,16,1024]{2,1,0:T(8,128)} async-done(((f32[6,16,1024]{2,1,0:T(8,128)}), f32[6,16,1024]{2,1,0:T(8,128)}) %all-reduce.3.cloned.1.call-update) | async-done | bytes 393232
  163.1 0.9 dynamic-slice_multiply_fusion
  164.1 31.7 %all_gather.3 = f32[6,16,1024]{2,0,1:T(8,128)S(1)} all-gather(f32[6,2,1024]{2,0,1:T(8,128)S(1)} %copy.41), channel_id=1, replica_groups=mesh['band'=4,'col'=8] {'col'}, dimensions={1}, use_global_device_ids=true | all-gather | bytes 442368 | tf_op jit(solution)/shard_map/all_gather | solution.py:105
  195.7 5.7 %fusion = f32[6,16,900]{2,1,0:T(8,128)} fusion(f32[900,512]{1,0:T(8,128)} %get-tuple-element.6, f32[900,512]{1,0:T(8,128)S(1)} %get-tuple-element.5, f32[6,16,1024]{2,0,1:T(8,128)S(1)} %all_gather.3), kind=kOutput, calls=%fused_computation.2 | convolution fusion | flops 1062604800 | bytes 4425216 | tf_op jit(solution)/shard_map/dot_general | solution.py:106
  (9 shorter events, 0.1 us)
Async XLA Ops:
  7.2 3.1 %copy-start = (bf16[6,16384]{1,0:T(8,128)(2,1)S(1)}, bf16[6,16384]{1,0:T(8,128)(2,1)}, u32[]{:S(2)}) copy-start(bf16[6,16384]{1,0:T(8,128)(2,1)} %param.6) | copy-start | bytes 589828
  16.1 0.7 copy-start.2
  18.4 4.9 %collective-permute-start = (f32[1,8,24,7,128]{4,2,3,1,0:T(8,128)S(1)}, f32[1,8,24,7,128]{4,2,3,1,0:T(8,128)}, u32[]{:S(2)}, u32[]{:S(2)}) collective-permute-start(f32[1,8,24,7,128]{4,2,3,1,0:T(8,128)S(1)} %copy.33), channel_id=1, source_target_pairs={{0,8},{8,16},{16,24},{1,9},{9,17},{17,25},{2,10},{10,18},{18,26},{... | collective-permute-start | bytes 2064392 | tf_op jit(solution)/shard_map/ppermute | solution.py:18
  21.9 5.5 %collective-permute-start.1 = (f32[1,8,24,7,128]{4,2,3,1,0:T(8,128)S(1)}, f32[1,8,24,7,128]{4,2,3,1,0:T(8,128)}, u32[]{:S(2)}, u32[]{:S(2)}) collective-permute-start(f32[1,8,24,7,128]{4,2,3,1,0:T(8,128)S(1)} %copy.34), channel_id=1, source_target_pairs={{8,0},{16,8},{24,16},{9,1},{17,9},{25,17},{10,2},{18,10},{26,18},{... | collective-permute-start | bytes 2064392 | tf_op jit(solution)/shard_map/ppermute | solution.py:19
  30.5 6.0 %copy-start.4 = (u32[32]{0:T(128)S(1)}, u32[32]{0:T(128)}, u32[]{:S(2)}) copy-start(u32[32]{0:T(128)} %constant.84) | copy-start | bytes 388
  30.5 51.4 %all-to-all-start = ((f32[3,8,24,7,128]{4,2,3,0,1:T(8,128)}), f32[3,8,24,7,128]{4,2,3,0,1:T(8,128)}, u32[]{:S(2)}, u32[]{:S(2)}) async-start(f32[3,8,24,7,128]{4,2,3,0,1:T(8,128)} %copy.37), calls=%async_computation | async-start | bytes 4128768 | tf_op jit(solution)/shard_map/all_to_all | solution.py:80
  36.4 126.6 %all-reduce.3.cloned.1.call-start = ((), (), s32[]{:S(2)}) async-start(), calls=%async_computation.1 | async-start | bytes 786432
  85.2 4.7 %copy-start.1 = (f32[6,16,900]{2,1,0:T(8,128)}, f32[6,16,900]{2,1,0:T(8,128)S(1)}, u32[]{:S(2)}) copy-start(f32[6,16,900]{2,1,0:T(8,128)S(1)} %reshape.113) | copy-start | bytes 1036804
  85.2 4.7 %copy-start.3 = (s32[2]{0:T(128)S(1)}, s32[2]{0:T(128)}, u32[]{:S(2)}) copy-start(s32[2]{0:T(128)} %param.11) | copy-start | bytes 28
Sparse Core Ops, SparseCore 0:
  90.1 72.9 all-reduce.2
where the time goes:
time: 209 us; the launch traced here: 208 us
  waiting for transfers between devices  111 us (53%)
  blocking collectives  31.7 us (15%)
  matrix products  17.2 us (8%)
  between operations  14.9 us (7%)
  other arithmetic  13.6 us (7%)
  starting transfers between devices  10.5 us (5%)
  local copies, waits for them, and re-layouts  9.29 us (4%)
    unnamed x2, waiting for transfers between devices  73.1 us
    all_to_all x1, waiting for transfers between devices, local(): lax.all_to_all(arranged, 'col', split_axis=1, concat_axis=1, tiled=True)  35.3 us
    all_gather x1, blocking collectives, local(): band_spectra = lax.all_gather(spectrum, 'col', axis=1, tiled=True)  31.7 us
    cos x1, other arithmetic, zonal_table(): return jnp.concatenate([jnp.cos(angles), jnp.sin(angles)], axis=1)  8.82 us
    all_to_all x1, starting transfers between devices, local(): lax.all_to_all(arranged, 'col', split_axis=1, concat_axis=1, tiled=True)  5.94 us
    dot_general x1, matrix products, local(): jnp.dot(band_spectra.reshape(levels * lat_band, 2 * KW), local_table.T, p...  5.74 us
    dot_general x1, matrix products, local(): jnp.einsum('lnb,nbt->nlt', picked, weights, preferred_element_type=jnp.fl...  4.73 us
    dot_general x1, matrix products, local(): jnp.dot(remapped.reshape(levels * lat_band, longitudes_here), local_table...  4.67 us
  transfers between devices with their start and end apart: 4, of which 3 were waited for; matrix products, arithmetic and copies ran while one was open for 5% of the time, Pallas kernels for 0%

commit v1 on v0

--- a/solution.py
+++ b/solution.py
@@ -102,7 +102,7 @@
     partial_spectra = partial_spectra.reshape(levels, lat_band, 2 * KW)
     spectrum = lax.psum_scatter(partial_spectra, "col", scatter_dimension=1, tiled=True)
     spectrum = spectrum * retained[None]
-    band_spectra = lax.all_gather(spectrum, "col", axis=1, tiled=True)
+    band_spectra = jnp.concatenate(lax.all_gather(spectrum, "col"), axis=1)
     filtered = jnp.dot(
         band_spectra.reshape(levels * lat_band, 2 * KW),
         local_table.T,

time: 209 us -> 209 us (level)
  no operation moved by 1% of the time
where the time goes in v1:
time: 209 us; the launch traced here: 208 us
  waiting for transfers between devices  111 us (53%)
  blocking collectives  31.4 us (15%)
  matrix products  17.1 us (8%)
  between operations  14.9 us (7%)
  other arithmetic  13.6 us (7%)
  starting transfers between devices  10.5 us (5%)
  local copies, waits for them, and re-layouts  9.57 us (5%)
    unnamed x2, waiting for transfers between devices  73 us
    all_to_all x1, waiting for transfers between devices, local(): lax.all_to_all(arranged, 'col', split_axis=1, concat_axis=1, tiled=True)  35.3 us
    all_gather x1, blocking collectives, local(): band_spectra = jnp.concatenate(lax.all_gather(spectrum, 'col'), axis=1)  31.4 us
    cos x1, other arithmetic, zonal_table(): return jnp.concatenate([jnp.cos(angles), jnp.sin(angles)], axis=1)  8.82 us
    all_to_all x1, starting transfers between devices, local(): lax.all_to_all(arranged, 'col', split_axis=1, concat_axis=1, tiled=True)  5.94 us
    dot_general x1, matrix products, local(): jnp.dot(band_spectra.reshape(levels * lat_band, 2 * KW), local_table.T, p...  5.64 us
    dot_general x1, matrix products, local(): jnp.einsum('lnb,nbt->nlt', picked, weights, preferred_element_type=jnp.fl...  4.73 us
    dot_general x1, matrix products, local(): jnp.dot(remapped.reshape(levels * lat_band, longitudes_here), local_table...  4.67 us
  transfers between devices with their start and end apart: 4, of which 3 were waited for; matrix products, arithmetic and copies ran while one was open for 5% of the time, Pallas kernels for 0%

profile of v1, /device:TPU:0, one launch (start us, length us, event | category | flops | bytes accessed | tf_op | source)
XLA Modules:
  0.0 208.2 jit_solution(5660498746091327981)
XLA Ops:
  7.2 0.0 copy-start
  7.2 0.7 compare_select_fusion.1
  7.9 0.7 compare_and_fusion
  8.6 0.9 convert_reduce_fusion
  9.5 0.7 convert_element_type.22
  10.2 0.0 copy-done
  10.2 0.8 gather_fusion
  11.0 4.7 %fusion.12 = f32[256,6,128]{2,1,0:T(8,128)S(1)} fusion(bf16[256,128,128]{2,1,0:T(8,128)(2,1)} %param.7, bf16[256,6,128]{2,1,0:T(8,128)(2,1)S(1)} %gather_fusion, pred[256]{0:T(512)(128)(4,1)S(1)} %compare_and_fusion), kind=kOutput, calls=%fused_computation.20 | convolution fusion | flops 50528256 | bytes 9568512 | tf_op jit(solution)/shard_map/lnb,nbt->nlt/dot_general | solution.py:56
  15.8 0.3 broadcast_in_dim.37
  16.1 0.0 copy-start.2
  16.1 0.2 pad_maximum_fusion.1
  16.4 0.4 copy.32
  16.7 0.1 copy-done.2
  16.8 1.2 fusion.11
  18.0 0.1 fusion.28
  18.2 0.1 slice.28
  18.3 0.1 copy.33
  18.4 3.3 %collective-permute-start = (f32[1,8,24,7,128]{4,2,3,1,0:T(8,128)S(1)}, f32[1,8,24,7,128]{4,2,3,1,0:T(8,128)}, u32[]{:S(2)}, u32[]{:S(2)}) collective-permute-start(f32[1,8,24,7,128]{4,2,3,1,0:T(8,128)S(1)} %copy.33), channel_id=1, source_target_pairs={{0,8},{8,16},{16,24},{1,9},{9,17},{17,25},{2,10},{10,18},{18,26},{... | collective-permute-start | bytes 2064392 | tf_op jit(solution)/shard_map/ppermute | solution.py:18
  21.7 0.1 slice.32
  21.8 0.1 copy.34
  21.9 1.3 collective-permute-start.1
  23.2 0.1 slice.30
  23.3 0.0 collective-permute-done
  23.3 1.2 copy.35
  24.6 2.8 %collective-permute-done.1 = f32[1,8,24,7,128]{4,2,3,1,0:T(8,128)} collective-permute-done((f32[1,8,24,7,128]{4,2,3,1,0:T(8,128)S(1)}, f32[1,8,24,7,128]{4,2,3,1,0:T(8,128)}, u32[]{:S(2)}, u32[]{:S(2)}) %collective-permute-start.1) | collective-permute-done | bytes 688160 | tf_op jit(solution)/shard_map/ppermute | solution.py:19
  27.4 1.2 copy.36
  28.6 0.2 pad_maximum_fusion
  28.9 1.7 copy.37
  30.5 5.9 %all-to-all-start = ((f32[3,8,24,7,128]{4,2,3,0,1:T(8,128)}), f32[3,8,24,7,128]{4,2,3,0,1:T(8,128)}, u32[]{:S(2)}, u32[]{:S(2)}) async-start(f32[3,8,24,7,128]{4,2,3,0,1:T(8,128)} %copy.37), calls=%async_computation | async-start | bytes 4128768 | tf_op jit(solution)/shard_map/all_to_all | solution.py:80
  36.4 0.0 all-reduce.3.cloned.1.call-start
  36.5 0.6 dynamic-slice
  37.8 8.8 %fusion.7 = (f32[900,512]{1,0:T(8,128)S(1)}, f32[900,512]{1,0:T(8,128)}) fusion(s32[900]{0:T(1024)S(1)} %iota_add_fusion), kind=kLoop, calls=%fused_computation.12 | loop fusion | flops 4147200 | bytes 3690000 | tf_op jit(solution)/shard_map/cos | solution.py:29
  46.6 35.3 %all-to-all-done = f32[3,8,24,7,128]{4,2,3,0,1:T(8,128)} async-done(((f32[3,8,24,7,128]{4,2,3,0,1:T(8,128)}), f32[3,8,24,7,128]{4,2,3,0,1:T(8,128)}, u32[]{:S(2)}, u32[]{:S(2)}) %all-to-all-start) | async-done | bytes 2064416 | tf_op jit(solution)/shard_map/all_to_all | solution.py:80
  81.9 1.8 copy.38
  83.7 0.2 fusion.16
  83.9 0.9 fusion.10
  84.8 0.1 copy.50
  84.9 0.3 reshape.115
  85.2 0.0 copy-start.1
  85.2 0.0 copy-start.3
  85.2 4.7 %fusion.1 = f32[6,16,1024]{2,1,0:T(8,128)} fusion(f32[6,16,900]{2,1,0:T(8,128)S(1)} %reshape.115, f32[900,512]{1,0:T(8,128)} %get-tuple-element.6, f32[900,512]{1,0:T(8,128)S(1)} %get-tuple-element.5), kind=kOutput, calls=%fused_computation.3 | convolution fusion | flops 1062604800 | bytes 4425216 | tf_op jit(solution)/shard_map/dot_general | solution.py:96
  89.9 0.0 all-reduce.3.cloned.1.call-update
  90.0 0.1 compare_select_fusion
  90.0 73.0 %all-reduce.3.cloned.1.call-done = f32[6,16,1024]{2,1,0:T(8,128)} async-done(((f32[6,16,1024]{2,1,0:T(8,128)}), f32[6,16,1024]{2,1,0:T(8,128)}) %all-reduce.3.cloned.1.call-update) | async-done | bytes 393232
  163.1 0.9 dynamic-slice_multiply_fusion
  164.0 31.4 %all-gather = f32[48,2,1024]{2,1,0:T(2,128)S(1)} all-gather(f32[6,2,1024]{2,1,0:T(2,128)S(1)} %dynamic-slice_multiply_fusion), channel_id=2, replica_groups=mesh['band'=4,'col'=8] {'col'}, dimensions={0}, use_global_device_ids=true | all-gather | bytes 442368 | tf_op jit(solution)/shard_map/all_gather | solution.py:105
  195.5 0.3 dot_general.27
  195.8 5.6 %fusion = f32[6,16,900]{2,1,0:T(8,128)} fusion(f32[6,16,1024]{2,1,0:T(8,128)S(1)} %dot_general.27, f32[900,512]{1,0:T(8,128)} %get-tuple-element.6, f32[900,512]{1,0:T(8,128)S(1)} %get-tuple-element.5), kind=kOutput, calls=%fused_computation.2 | convolution fusion | flops 1062604800 | bytes 4425216 | tf_op jit(solution)/shard_map/dot_general | solution.py:106
  (10 shorter events, 0.1 us)
Async XLA Ops:
  7.2 3.1 %copy-start = (bf16[6,16384]{1,0:T(8,128)(2,1)S(1)}, bf16[6,16384]{1,0:T(8,128)(2,1)}, u32[]{:S(2)}) copy-start(bf16[6,16384]{1,0:T(8,128)(2,1)} %param.6) | copy-start | bytes 589828
  16.1 0.7 copy-start.2
  18.4 4.9 %collective-permute-start = (f32[1,8,24,7,128]{4,2,3,1,0:T(8,128)S(1)}, f32[1,8,24,7,128]{4,2,3,1,0:T(8,128)}, u32[]{:S(2)}, u32[]{:S(2)}) collective-permute-start(f32[1,8,24,7,128]{4,2,3,1,0:T(8,128)S(1)} %copy.33), channel_id=1, source_target_pairs={{0,8},{8,16},{16,24},{1,9},{9,17},{17,25},{2,10},{10,18},{18,26},{... | collective-permute-start | bytes 2064392 | tf_op jit(solution)/shard_map/ppermute | solution.py:18
  21.9 5.5 %collective-permute-start.1 = (f32[1,8,24,7,128]{4,2,3,1,0:T(8,128)S(1)}, f32[1,8,24,7,128]{4,2,3,1,0:T(8,128)}, u32[]{:S(2)}, u32[]{:S(2)}) collective-permute-start(f32[1,8,24,7,128]{4,2,3,1,0:T(8,128)S(1)} %copy.34), channel_id=1, source_target_pairs={{8,0},{16,8},{24,16},{9,1},{17,9},{25,17},{10,2},{18,10},{26,18},{... | collective-permute-start | bytes 2064392 | tf_op jit(solution)/shard_map/ppermute | solution.py:19
  30.5 6.0 %copy-start.4 = (u32[32]{0:T(128)S(1)}, u32[32]{0:T(128)}, u32[]{:S(2)}) copy-start(u32[32]{0:T(128)} %constant.84) | copy-start | bytes 388
  30.5 51.4 %all-to-all-start = ((f32[3,8,24,7,128]{4,2,3,0,1:T(8,128)}), f32[3,8,24,7,128]{4,2,3,0,1:T(8,128)}, u32[]{:S(2)}, u32[]{:S(2)}) async-start(f32[3,8,24,7,128]{4,2,3,0,1:T(8,128)} %copy.37), calls=%async_computation | async-start | bytes 4128768 | tf_op jit(solution)/shard_map/all_to_all | solution.py:80
  36.4 126.6 %all-reduce.3.cloned.1.call-start = ((), (), s32[]{:S(2)}) async-start(), calls=%async_computation.1 | async-start | bytes 786432
  85.2 4.7 %copy-start.1 = (f32[6,16,900]{2,1,0:T(8,128)}, f32[6,16,900]{2,1,0:T(8,128)S(1)}, u32[]{:S(2)}) copy-start(f32[6,16,900]{2,1,0:T(8,128)S(1)} %reshape.115) | copy-start | bytes 1036804
  85.2 4.7 %copy-start.3 = (s32[2]{0:T(128)S(1)}, s32[2]{0:T(128)}, u32[]{:S(2)}) copy-start(s32[2]{0:T(128)} %param.11) | copy-start | bytes 28
Sparse Core Ops, SparseCore 0:
  90.1 72.9 all-reduce.2
